TPU v7x, 32 devices: a whole 2x2x4 slice. The times are simulated.
32 devices in a mesh: tm: 8 (over z, core), member: 4 (over y, x).
Axes of the slice: x: 2, y: 2, z: 4, core: 2. Of those that a mesh axis runs over, the one named last changes fastest.
Arguments:
- fields: float32 [48, 48, 8192], P('member', 'tm'), may hold values from 200 to 350, as said below
Outputs:
- covariance: float32 [48, 48, 8192], P('member', None, 'tm')
Inputs may be any that keep to these rules, and one draw needn't show every extreme that they name: `fields`: month t is calendar month t mod 12.
All inputs are finite; a program needn't handle non-finite values.
Results may differ from a plain program's by a relative error of at most 0.0003.
Values sent between devices are 32-bit elements; how exact they have to be, the bound alone decides.
A program may use at most 192 MiB of HBM per device.

v0:
```python
import jax
import jax.numpy as jnp
from jax import lax
from jax.sharding import PartitionSpec as P


def monthly_anomaly(series):
    members_here, months_here, pixel_count = series.shape
    by_year = series.reshape(members_here, months_here // 12, 12, pixel_count)
    climatology = jnp.mean(by_year, axis=1, keepdims=True)
    return (by_year - climatology).reshape(members_here, months_here, pixel_count)


def cross_block(first_rows, second_rows, divisor):
    products = jnp.einsum(
        "itp,jtp->ijp",
        first_rows,
        second_rows,
        precision=lax.Precision.HIGHEST,
        preferred_element_type=jnp.float32,
    )
    return products / divisor


def per_device(fields):
    members_here, mon_here, pixel_count = fields.shape
    tm_count = lax.axis_size("tm")
    divisor = float(mon_here * tm_count - 12)
    regrouped = lax.all_to_all(
        lax.all_to_all(fields, "tm", split_axis=2, concat_axis=1, tiled=True),
        "member",
        split_axis=2,
        concat_axis=0,
        tiled=True,
    )
    anomaly = monthly_anomaly(regrouped)
    whole_block = cross_block(anomaly, anomaly, divisor)
    return lax.all_to_all(whole_block, "member", split_axis=0, concat_axis=2, tiled=True)


def solution(mesh):
    in_specs = (P("member", "tm", None),)
    out_specs = P("member", None, "tm")
    return jax.shard_map(
        per_device, mesh=mesh, in_specs=in_specs, out_specs=out_specs, check_vma=False
    )
```

profile of v0, /device:TPU:0, one launch (start us, length us, event | category | flops | bytes accessed | tf_op | source)
XLA Modules:
  0.0 288.6 jit_solution(1620361578068104155)
XLA Ops:
  0.0 17.2 %copy.42 = f32[12,6,8192]{0,1,2:T(8,128)} copy(f32[12,6,8192]{2,1,0:T(8,128)} %param.1) | data formatting | bytes 4718592 | tf_op args[0]
  17.2 18.9 %reshape.15 = f32[8,1,73728]{2,1,0:T(1,128)S(1)} reshape(f32[8192,6,12]{2,1,0:T(8,128)} %bitcast.24) | data formatting | bytes 4718592
  36.2 60.9 %all_to_all.51 = f32[8,1,73728]{2,1,0:T(1,128)} all-to-all(f32[8,1,73728]{2,1,0:T(1,128)S(1)} %reshape.15), channel_id=1, replica_groups=mesh['tm'=8,'member'=4] {'tm'}, dimensions={0} | all-to-all | bytes 4718592 | tf_op jit(solution)/shard_map/all_to_all | solution.py:30
  97.1 0.6 broadcast.10
  97.6 7.9 %reduce.1 = f32[8,73728]{1,0:T(8,128)S(1)} reduce(f32[8,1,73728]{2,1,0:T(1,128)} %all_to_all.51, f32[]{:T(128)} %broadcast.10), dimensions={1}, to_apply=%all_to_all.37.reduce_sub_computation | reduce | bytes 4718596 | tf_op jit(solution)/shard_map/all_to_all | solution.py:30
  105.6 26.9 %reshape.16 = f32[8192,6,12]{2,1,0:T(8,128)} reshape(f32[8,73728]{1,0:T(8,128)S(1)} %reduce.1) | data formatting | bytes 4718592
  132.4 19.7 %copy.43 = f32[12,6,8,1024]{3,1,2,0:T(8,128)S(1)} copy(f32[12,6,8,1024]{0,1,3,2:T(8,128)} %bitcast.23) | data formatting | bytes 4718592 | tf_op jit(solution)/shard_map/all_to_all | solution.py:30
  152.1 1.6 all_to_all.40
  153.7 7.6 %copy.44 = f32[12,48,1024]{1,0,2:T(8,128)} copy(f32[12,48,1024]{2,1,0:T(8,128)} %all_to_all.40) | data formatting | bytes 4718592 | tf_op jit(solution)/shard_map/all_to_all | solution.py:30
  161.3 8.8 %reshape.17 = f32[4,1,147456]{2,1,0:T(1,128)} reshape(f32[1024,12,48]{2,1,0:T(8,128)} %bitcast.25) | data formatting | bytes 4718592
  170.1 32.1 %all_to_all.52 = f32[4,1,147456]{2,1,0:T(1,128)S(1)} all-to-all(f32[4,1,147456]{2,1,0:T(1,128)} %reshape.17), channel_id=1, replica_groups=mesh['tm'=8,'member'=4] {'member'}, dimensions={0} | all-to-all | bytes 4718592 | tf_op jit(solution)/shard_map/all_to_all | solution.py:29
  202.1 8.3 %reduce.2 = f32[4,147456]{1,0:T(4,128)} reduce(f32[4,1,147456]{2,1,0:T(1,128)S(1)} %all_to_all.52, f32[]{:T(128)} %broadcast.10), dimensions={1}, to_apply=%all_to_all.41.reduce_sub_computation | reduce | bytes 4718596 | tf_op jit(solution)/shard_map/all_to_all | solution.py:29
  210.4 10.3 %reshape.18 = f32[1024,12,48]{2,1,0:T(8,128)} reshape(f32[4,147456]{1,0:T(4,128)} %reduce.2) | data formatting | bytes 4718592
  220.7 5.7 %copy.54 = f32[12,48,4,256]{3,2,1,0:T(4,128)S(1)} copy(f32[12,48,4,256]{1,0,3,2:T(8,128)} %bitcast.26) | data formatting | bytes 4718592 | tf_op jit(solution)/shard_map/all_to_all | solution.py:29
  226.4 0.8 reduce
  227.3 0.4 copy_multiply_fusion
  227.7 0.5 copy.46
  228.2 0.3 sub.11
  228.4 1.4 bitcast_subtract_fusion
  229.9 5.4 %copy.50 = f32[48,48,256]{1,0,2:T(8,128)} copy(f32[48,48,256]{2,1,0:T(8,128)S(1)} %bitcast_subtract_fusion) | data formatting | bytes 4718592 | tf_op jit(solution)/shard_map/sub | solution.py:11
  235.2 16.4 %multiply_bitcast_fusion = f32[48,48,256]{0,1,2:T(8,128)} fusion(f32[48,48,256]{1,0,2:T(8,128)} %copy.50), kind=kOutput, calls=%fused_computation | convolution fusion | flops 340328448 | bytes 4718592 | tf_op jit(solution)/shard_map/itp,jtp->ijp/dot_general | solution.py:15
  251.6 5.9 %copy.52 = f32[48,48,256]{2,1,0:T(8,128)S(1)} copy(f32[48,48,256]{0,1,2:T(8,128)} %multiply_bitcast_fusion) | data formatting | bytes 4718592 | tf_op jit(solution)/shard_map/div | solution.py:22
  257.5 29.3 %all_to_all.53 = f32[48,48,256]{2,1,0:T(8,128)S(1)} all-to-all(f32[48,48,256]{2,1,0:T(8,128)S(1)} %copy.52), channel_id=1, replica_groups=mesh['tm'=8,'member'=4] {'member'}, dimensions={0} | all-to-all | bytes 4718592 | tf_op jit(solution)/shard_map/all_to_all | solution.py:38
  286.8 1.7 copy.56
  (1 shorter events, 0.1 us)
where the time goes:
time: 293 us; the launch traced here: 289 us
  local copies, waits for them, and re-layouts  131 us (45%)
  blocking collectives  122 us (42%)
  other arithmetic  18.8 us (6%)
  matrix products  16.4 us (6%)
    unnamed x6, local copies, waits for them, and re-layouts  82.2 us
    all_to_all x1, blocking collectives, per_device(): lax.all_to_all(fields, 'tm', split_axis=2, concat_axis=1, tiled=True)  60.9 us
    all_to_all x1, blocking collectives, per_device(): lax.all_to_all(lax.all_to_all(fields, 'tm', split_axis=2, concat_axis=1,...  32.1 us
    all_to_all x4, local copies, waits for them, and re-layouts, per_device(): lax.all_to_all(fields, 'tm', split_axis=2, concat_axis=1, tiled=True)  29.4 us
    all_to_all x1, blocking collectives, per_device(): lax.all_to_all(whole_block, 'member', split_axis=0, concat_axis=2, tiled=...  29.3 us
    dot_general x1, matrix products, cross_block(): jnp.einsum('itp,jtp->ijp', first_rows, second_rows, precision=lax.Precisi...  16.4 us
    all_to_all x1, other arithmetic, per_device(): lax.all_to_all(lax.all_to_all(fields, 'tm', split_axis=2, concat_axis=1,...  8.3 us
    all_to_all x1, other arithmetic, per_device(): lax.all_to_all(fields, 'tm', split_axis=2, concat_axis=1, tiled=True)  7.95 us

commit v1 on v0

v1 whole, which is shorter than its diff:
```python
import functools
import math

import jax
import jax.numpy as jnp
from jax import lax
from jax.experimental import pallas as pl
from jax.experimental.pallas import tpu as pltpu
from jax.sharding import PartitionSpec as P

MESH = pl.DeviceIdType.MESH
LANES = 128
YEAR = 12


def contrasts(series, divisor):
    count = len(series)
    if count & (count - 1):
        mean = sum(series[1:], series[0]) * (1.0 / count)
        return [(s - mean) * (1.0 / math.sqrt(divisor)) for s in series]
    found, width = [], 1
    while len(series) > 1:
        width *= 2
        scale = 1.0 / math.sqrt(width * divisor)
        found += [(p - q) * scale for p, q in zip(series[::2], series[1::2])]
        series = [p + q for p, q in zip(series[::2], series[1::2])]
    return found


def kernel(dims, x_ref, out_ref, packed, landed, every, rows_of, cov, fsend, frecv, csend, crecv, own_sem):
    tms, groups, chunks, members, months, years = dims
    devices = tms * groups
    parts = YEAR // months
    terms = rows_of.shape[1]
    total = every.shape[1]
    a, b = lax.axis_index("tm"), lax.axis_index("member")
    me = a * groups + b

    def device(index):
        return (index // groups, lax.rem(index, groups))

    barrier = pltpu.get_barrier_semaphore()

    def greet(d, _):
        pl.semaphore_signal(
            barrier, inc=1, device_id=device(lax.rem(me + d, devices)), device_id_type=MESH
        )
        return 0

    lax.fori_loop(1, devices, greet, 0)

    def field_copy(k, source, dest, target):
        return pltpu.make_async_remote_copy(
            src_ref=packed.at[k, dest],
            dst_ref=landed.at[k, source],
            send_sem=fsend.at[k, dest],
            recv_sem=frecv.at[k, source],
            device_id=device(target),
            device_id_type=MESH,
        )

    def pack(dest, _):
        for k in range(chunks):
            columns = pl.ds(pl.multiple_of((dest * chunks + k) * LANES, LANES), LANES)
            for m in range(members):
                packed[k, dest, pl.ds(m, months, stride=members), :] = x_ref[m, :, columns]
        return 0

    lax.fori_loop(0, devices, pack, 0)
    pl.semaphore_wait(barrier, devices - 1)

    for k in range(chunks):

        def send(d, _):
            dest = lax.rem(me + d, devices)
            field_copy(k, me, dest, dest).start()
            return 0

        half = devices // 2
        lax.fori_loop(half, devices, send, 0)
        lax.fori_loop(1, half, send, 0)
        landed[k, me] = packed[k, me]

    def cov_copy(k, offset):
        return pltpu.make_async_remote_copy(
            src_ref=cov.at[k, offset],
            dst_ref=out_ref.at[:, :, pl.ds(pl.multiple_of((b * chunks + k) * LANES, LANES), LANES)],
            send_sem=csend.at[k, offset],
            recv_sem=crecv.at[k, offset],
            device_id=(a, lax.rem(b + offset, groups)),
            device_id_type=MESH,
        )

    def own_copy(k):
        return pltpu.make_async_copy(
            cov.at[k, 0],
            out_ref.at[:, :, pl.ds(pl.multiple_of((b * chunks + k) * LANES, LANES), LANES)],
            own_sem.at[k],
        )

    for k in range(chunks):

        def arrive(d, _):
            source = lax.rem(me + d, devices)
            field_copy(k, source, source, source).wait_recv()
            return 0

        lax.fori_loop(1, devices, arrive, 0)

        for part in range(parts):
            for g in range(groups):
                for c in range(months):
                    series = [
                        landed[k, (y * parts + part) * groups + g, c * members : (c + 1) * members, :]
                        for y in range(years)
                    ]
                    for q, u in enumerate(contrasts(series, float(years * YEAR - YEAR))):
                        t = (q * parts + part) * months + c
                        every[t, g * members : (g + 1) * members, :] = u
                        rows_of[g, t] = u

        for offset in list(range(1, groups)) + [0]:
            target = lax.rem(b + offset, groups)
            for first in range(0, total, 16):
                tiles = range(first, min(first + 16, total), 8)

                def step(t, sums):
                    across = [every[t, j : j + 8, :] for j in tiles]
                    new = []
                    for i in range(members):
                        row = jnp.broadcast_to(rows_of[target, t, i : i + 1, :], (8, LANES))
                        for n, v in enumerate(across):
                            new.append(sums[i * len(across) + n] + row * v)
                    return tuple(new)

                zero = jnp.zeros((8, LANES), jnp.float32)
                sums = lax.fori_loop(0, terms, step, (zero,) * (members * len(tiles)), unroll=2)
                for i in range(members):
                    for n, j in enumerate(tiles):
                        cov[k, offset, i, j : j + 8, :] = sums[i * len(tiles) + n]
            if offset:
                cov_copy(k, offset).start()
            else:
                own_copy(k).start()

    for k in range(chunks):

        def sent(d, _):
            dest = lax.rem(me + d, devices)
            field_copy(k, me, dest, dest).wait_send()
            return 0

        lax.fori_loop(1, devices, sent, 0)
        own_copy(k).wait()
        for offset in range(1, groups):
            cov_copy(k, offset).wait()


def solution(mesh):
    tms, groups = mesh.shape["tm"], mesh.shape["member"]

    def per_device(fields):
        members, months, pixels = fields.shape
        devices = tms * groups
        chunks = pixels // (devices * LANES)
        years = months * tms // YEAR
        terms = (years if years & (years - 1) else years - 1) * YEAR
        total = members * groups
        here = pixels // tms
        dims = (tms, groups, chunks, members, months, years)
        rows = members * months
        return pl.pallas_call(
            functools.partial(kernel, dims),
            out_shape=jax.ShapeDtypeStruct((members, total, here), jnp.float32),
            in_specs=[pl.BlockSpec(memory_space=pltpu.VMEM)],
            out_specs=pl.BlockSpec(memory_space=pl.ANY),
            scratch_shapes=[
                pltpu.VMEM((chunks, devices, rows, LANES), jnp.float32),
                pltpu.VMEM((chunks, devices, rows, LANES), jnp.float32),
                pltpu.VMEM((terms, total, LANES), jnp.float32),
                pltpu.VMEM((groups, terms, members, LANES), jnp.float32),
                pltpu.VMEM((chunks, groups, members, total, LANES), jnp.float32),
                pltpu.SemaphoreType.DMA((chunks, devices)),
                pltpu.SemaphoreType.DMA((chunks, devices)),
                pltpu.SemaphoreType.DMA((chunks, groups)),
                pltpu.SemaphoreType.DMA((chunks, groups)),
                pltpu.SemaphoreType.DMA((chunks,)),
            ],
            compiler_params=pltpu.CompilerParams(
                collective_id=0, has_side_effects=True, vmem_limit_bytes=48 * 1024 * 1024
            ),
        )(fields)

    return jax.shard_map(
        per_device,
        mesh=mesh,
        in_specs=(P("member", "tm", None),),
        out_specs=P("member", None, "tm"),
        check_vma=False,
    )
```

time: 293 us -> 80.1 us (0.27); the launches traced: 289 us -> 80 us
  local copies, waits for them, and re-layouts: 131 us -> 3.3 us
  blocking collectives: 122 us -> 0 us
  Pallas kernels: 0 us -> 76.7 us
  other arithmetic: 18.8 us -> 0 us
  matrix products: 16.4 us -> 0 us
    all_to_all x3 -> x0, blocking collectives: 122 us -> none  [the longest x1 60.9 us: per_device(): lax.all_to_all(fields, 'tm', split_axis=2, concat_axis=1, tiled=True)]
    unnamed x6 -> x3, local copies, waits for them, and re-layouts: 82.2 us -> 3.3 us
    pallas_call x0 -> x1, Pallas kernels: none -> 76.7 us  [per_device(): pl.pallas_call(functools.partial(kernel, dims), out_shape=jax.ShapeDtypeS...]
    all_to_all x7 -> x0, local copies, waits for them, and re-layouts: 37.2 us -> none  [the longest x4 29.4 us: per_device(): lax.all_to_all(fields, 'tm', split_axis=2, concat_axis=1, tiled=True)]
    dot_general x1 -> x0, matrix products: 16.4 us -> none  [cross_block(): jnp.einsum('itp,jtp->ijp', first_rows, second_rows, precision=lax.Precisi...]
    all_to_all x2 -> x0, other arithmetic: 16.2 us -> none  [the longest x1 8.3 us: per_device(): lax.all_to_all(lax.all_to_all(fields, 'tm', split_axis=2, concat_axis=1,...]
    div x1 -> x0, local copies, waits for them, and re-layouts: 5.86 us -> none  [cross_block(): return products / divisor]
    sub x2 -> x0, local copies, waits for them, and re-layouts: 5.64 us -> none  [monthly_anomaly(): by_year - climatology]
where the time goes in v1:
time: 80.1 us; the launch traced here: 80 us
  Pallas kernels  76.7 us (96%)
  local copies, waits for them, and re-layouts  3.3 us (4%)
    pallas_call x1, Pallas kernels, per_device(): pl.pallas_call(functools.partial(kernel, dims), out_shape=jax.ShapeDtypeS...  76.7 us
    unnamed x3, local copies, waits for them, and re-layouts  3.3 us

profile of v1, /device:TPU:0, one launch (start us, length us, event | category | flops | bytes accessed | tf_op | source)
XLA Modules:
  0.0 80.0 jit_solution(14108631905854096666)
XLA Ops:
  0.0 0.0 copy-start
  0.0 1.9 %copy-done = f32[12,6,8192]{2,1,0:T(8,128)S(1)} copy-done((f32[12,6,8192]{2,1,0:T(8,128)S(1)}, f32[12,6,8192]{2,1,0:T(8,128)}, u32[]{:S(2)}) %copy-start) | copy-done | bytes 2359320
  1.9 76.7 %shard_map.17 = f32[12,48,1024]{2,1,0:T(8,128)S(1)} custom-call(f32[12,6,8192]{2,1,0:T(8,128)S(1)} %copy-done), custom_call_target="tpu_custom_call" | custom-call | tf_op jit(solution)/shard_map/pallas_call | solution.py:172
  78.6 1.4 %copy.3 = f32[12,48,1024]{2,1,0:T(8,128)} copy(f32[12,48,1024]{2,1,0:T(8,128)S(1)} %shard_map.17) | data formatting | bytes 4718592
Async XLA Ops:
  0.0 1.9 %copy-start = (f32[12,6,8192]{2,1,0:T(8,128)S(1)}, f32[12,6,8192]{2,1,0:T(8,128)}, u32[]{:S(2)}) copy-start(f32[12,6,8192]{2,1,0:T(8,128)} %x_ref.1) | copy-start | bytes 7077892

commit v2 on v1

v2 whole, which is shorter than its diff:
```python
import functools
import math

import jax
import jax.numpy as jnp
from jax import lax
from jax.experimental import pallas as pl
from jax.experimental.pallas import tpu as pltpu
from jax.sharding import PartitionSpec as P

MESH = pl.DeviceIdType.MESH
LANES = 128
YEAR = 12


def contrasts(series, divisor):
    count = len(series)
    if count & (count - 1):
        mean = sum(series[1:], series[0]) * (1.0 / count)
        return [(s - mean) * (1.0 / math.sqrt(divisor)) for s in series]
    found, width = [], 1
    while len(series) > 1:
        width *= 2
        scale = 1.0 / math.sqrt(width * divisor)
        found += [(p - q) * scale for p, q in zip(series[::2], series[1::2])]
        series = [p + q for p, q in zip(series[::2], series[1::2])]
    return found


def kernel(
    dims, x_hbm, out_ref, x_ref, packed, landed, every, rows_of, cov, halves, halves_in,
    xsem, fsend, frecv, csend, crecv,
):
    tms, groups, chunks, members, months, years, folded = dims
    devices = tms * groups
    parts = YEAR // months
    terms = rows_of.shape[1]
    total = every.shape[1]
    rows = members * months
    split = -(-rows // 16) * 8
    here = out_ref.shape[2]
    a, b = lax.axis_index("tm"), lax.axis_index("member")
    me = a * groups + b
    low = lax.broadcasted_iota(jnp.int32, (8, LANES), 1) < LANES // 2
    stages = [(k, None, 0, rows) for k in range(chunks)]
    if folded:
        stages[-1:] = [(chunks - 1, 0, 0, split), (chunks - 1, 1, split, rows)]

    def device(index):
        return (index // groups, lax.rem(index, groups))

    def piece(block):
        pixels = pl.ds(pl.multiple_of(block * here, LANES), here)
        return pltpu.make_async_copy(x_hbm.at[:, :, pixels], x_ref.at[:, :, pixels], xsem.at[block])

    def load(n, _):
        piece(lax.rem(a + tms // 2 + n, tms)).start()
        return 0

    lax.fori_loop(0, tms, load, 0)
    barrier = pltpu.get_barrier_semaphore()

    def greet(d, _):
        pl.semaphore_signal(
            barrier, inc=1, device_id=device(lax.rem(me + d, devices)), device_id_type=MESH
        )
        return 0

    lax.fori_loop(1, devices, greet, 0)

    def field_copy(s, source, dest):
        k, _, first, last = stages[s]
        return pltpu.make_async_remote_copy(
            src_ref=packed.at[k, dest, pl.ds(first, last - first)],
            dst_ref=landed.at[k, source, pl.ds(first, last - first)],
            send_sem=fsend.at[s, dest],
            recv_sem=frecv.at[s, source],
            device_id=device(dest),
            device_id_type=MESH,
        )

    def swap(v):
        return pltpu.roll(v, LANES // 2, 1)

    def pack(k, half, dest):
        columns = pl.ds(pl.multiple_of((dest * chunks + k) * LANES, LANES), LANES)
        for m in range(members):
            if half is None:
                packed[k, dest, pl.ds(m, months, stride=members), :] = x_ref[m, :, columns]
            else:
                cut = months // 2
                p, q = x_ref[m, :cut, columns], x_ref[m, cut:, columns]
                mask = lax.broadcasted_iota(jnp.int32, p.shape, 1) < LANES // 2
                packed[k, dest, pl.ds(m, cut, stride=members), :] = jnp.where(mask, p, swap(q))
                packed[k, dest, pl.ds(rows // 2 + m, cut, stride=members), :] = jnp.where(mask, swap(p), q)

    for s, (k, half, _, _) in enumerate(stages):

        def block(n, _):
            to = lax.rem(a + tms // 2 + n, tms)
            if s == 0:
                piece(to).wait()
            if not half:

                def pack_one(g, _):
                    pack(k, half, to * groups + g)
                    return 0

                lax.fori_loop(0, groups, pack_one, 0)
            if s == 0:

                @pl.when(n == 0)
                def _():
                    pl.semaphore_wait(barrier, devices - 1)

            def send(g, _):
                dest = to * groups + lax.rem(b + g, groups)

                @pl.when(dest != me)
                def _():
                    field_copy(s, me, dest).start()

                return 0

            lax.fori_loop(0, groups, send, 0)
            return 0

        lax.fori_loop(0, tms, block, 0)
    for k in range(chunks):
        landed[k, me] = packed[k, me]

    def columns_of(k, group):
        return pl.ds(pl.multiple_of((group * chunks + k) * LANES, LANES), LANES)

    def cov_copy(s, offset):
        k, half, _, _ = stages[s]
        return pltpu.make_async_remote_copy(
            src_ref=cov.at[k, offset - 1] if half is None else halves.at[half, offset],
            dst_ref=out_ref.at[:, :, columns_of(k, b)] if half is None else halves_in.at[half, offset],
            send_sem=csend.at[s, offset],
            recv_sem=crecv.at[s, offset],
            device_id=(a, lax.rem(b + offset, groups)),
            device_id_type=MESH,
        )

    for s, (k, half, _, _) in enumerate(stages):

        def arrive(d, _):
            source = lax.rem(me + d, devices)
            field_copy(s, source, source).wait_recv()
            return 0

        lax.fori_loop(1, devices, arrive, 0)
        spans = months if half is None else months // 2
        base = rows // 2 if half else 0
        for part in range(parts):
            for g in range(groups):
                for c in range(spans):
                    at = base + c * members
                    series = [
                        landed[k, (y * parts + part) * groups + g, at : at + members, :]
                        for y in range(years)
                    ]
                    for q, u in enumerate(contrasts(series, float(years * YEAR - YEAR))):
                        t = (q * parts + part) * spans + c
                        every[t, g * members : (g + 1) * members, :] = u
                        rows_of[g, t] = u

        for offset in list(range(1, groups)) + [0]:
            target = lax.rem(b + offset, groups)
            for first in range(0, total, 16):
                tiles = range(first, min(first + 16, total), 8)

                def step(t, sums):
                    across = [every[t, j : j + 8, :] for j in tiles]
                    new = []
                    for i in range(members):
                        row = jnp.broadcast_to(rows_of[target, t, i : i + 1, :], (8, LANES))
                        for n, v in enumerate(across):
                            new.append(sums[i * len(across) + n] + row * v)
                    return tuple(new)

                zero = jnp.zeros((8, LANES), jnp.float32)
                used = terms if half is None else terms // 2
                sums = lax.fori_loop(0, used, step, (zero,) * (members * len(tiles)), unroll=2)
                for n, j in enumerate(tiles):
                    got = sums[n :: len(tiles)]
                    if half is not None:
                        for p in range(members // 2):
                            u, v = got[2 * p + half], got[2 * p + 1 - half]
                            halves[half, offset, p, j : j + 8, :] = jnp.where(low, u, v) + swap(
                                jnp.where(low, v, u)
                            )
                    elif offset:
                        for i in range(members):
                            cov[k, offset - 1, i, j : j + 8, :] = got[i]
                    else:
                        for i in range(members):
                            out_ref[i, j : j + 8, columns_of(k, b)] = got[i]
            if offset:
                cov_copy(s, offset).start()

    if folded:
        s, k = len(stages) - 1, chunks - 1
        for offset in range(groups):
            for half in range(2):
                if offset:
                    cov_copy(s - 1 + half, offset).wait_recv()
            here_in = halves_in if offset else halves
            columns = columns_of(k, lax.rem(b + groups - offset, groups))

            def unpack(p, _):
                for j in range(0, total, 8):
                    u, v = here_in[0, offset, p, j : j + 8, :], here_in[1, offset, p, j : j + 8, :]
                    out_ref[2 * p, j : j + 8, columns] = jnp.where(low, u, v)
                    out_ref[2 * p + 1, j : j + 8, columns] = swap(jnp.where(low, v, u))
                return 0

            lax.fori_loop(0, members // 2, unpack, 0)

    for s, (k, half, _, _) in enumerate(stages):

        def sent(d, _):
            field_copy(s, me, lax.rem(me + d, devices)).wait_send()
            return 0

        lax.fori_loop(1, devices, sent, 0)
        for offset in range(1, groups):
            if half is None:
                cov_copy(s, offset).wait_recv()
            cov_copy(s, offset).wait_send()


def solution(mesh):
    tms, groups = mesh.shape["tm"], mesh.shape["member"]

    def per_device(fields):
        members, months, pixels = fields.shape
        devices = tms * groups
        chunks = pixels // (devices * LANES)
        years = months * tms // YEAR
        terms = (years if years & (years - 1) else years - 1) * YEAR
        total = members * groups
        here = pixels // tms
        rows = members * months
        folded = rows % 8 == 0 and months % 2 == 0 and members % 2 == 0
        dims = (tms, groups, chunks, members, months, years, folded)
        stages = chunks + folded
        pairs = members // 2 if folded else 1
        return pl.pallas_call(
            functools.partial(kernel, dims),
            out_shape=jax.ShapeDtypeStruct((members, total, here), jnp.float32),
            in_specs=[pl.BlockSpec(memory_space=pltpu.HBM)],
            out_specs=pl.BlockSpec(memory_space=pltpu.VMEM),
            scratch_shapes=[
                pltpu.VMEM((members, months, pixels), jnp.float32),
                pltpu.VMEM((chunks, devices, rows, LANES), jnp.float32),
                pltpu.VMEM((chunks, devices, rows, LANES), jnp.float32),
                pltpu.VMEM((terms, total, LANES), jnp.float32),
                pltpu.VMEM((groups, terms, members, LANES), jnp.float32),
                pltpu.VMEM((chunks, groups - 1, members, total, LANES), jnp.float32),
                pltpu.VMEM((2, groups, pairs, total, LANES), jnp.float32),
                pltpu.VMEM((2, groups, pairs, total, LANES), jnp.float32),
                pltpu.SemaphoreType.DMA((tms,)),
                pltpu.SemaphoreType.DMA((stages, devices)),
                pltpu.SemaphoreType.DMA((stages, devices)),
                pltpu.SemaphoreType.DMA((stages, groups)),
                pltpu.SemaphoreType.DMA((stages, groups)),
            ],
            compiler_params=pltpu.CompilerParams(
                collective_id=0, has_side_effects=True, vmem_limit_bytes=48 * 1024 * 1024
            ),
        )(fields)

    return jax.shard_map(
        per_device,
        mesh=mesh,
        in_specs=(P("member", "tm", None),),
        out_specs=P("member", None, "tm"),
        check_vma=False,
    )
```

time: 80.1 us -> 78.3 us (0.978); the launches traced: 80 us -> 77.3 us
  Pallas kernels: 76.7 us -> 74 us
    pallas_call x1, Pallas kernels: 76.7 us -> 74 us  [per_device(): pl.pallas_call(functools.partial(kernel, dims), out_shape=jax.ShapeDtypeS...]
where the time goes in v2:
time: 78.3 us; the launch traced here: 77.3 us
  Pallas kernels  74 us (95%)
  local copies, waits for them, and re-layouts  3.3 us (4%)
    pallas_call x1, Pallas kernels, per_device(): pl.pallas_call(functools.partial(kernel, dims), out_shape=jax.ShapeDtypeS...  74 us
    unnamed x3, local copies, waits for them, and re-layouts  3.3 us

profile of v2, /device:TPU:0, one launch (start us, length us, event | category | flops | bytes accessed | tf_op | source)
XLA Modules:
  0.0 77.3 jit_solution(3848968326044696743)
XLA Ops:
  0.0 0.0 copy-start
  0.0 1.9 %copy-done = f32[12,6,8192]{2,1,0:T(8,128)S(1)} copy-done((f32[12,6,8192]{2,1,0:T(8,128)S(1)}, f32[12,6,8192]{2,1,0:T(8,128)}, u32[]{:S(2)}) %copy-start) | copy-done | bytes 2359320
  1.9 74.0 %shard_map.17 = f32[12,48,1024]{2,1,0:T(8,128)S(1)} custom-call(f32[12,6,8192]{2,1,0:T(8,128)S(1)} %copy-done), custom_call_target="tpu_custom_call" | custom-call | tf_op jit(solution)/shard_map/pallas_call | solution.py:250
  75.9 1.4 %copy.3 = f32[12,48,1024]{2,1,0:T(8,128)} copy(f32[12,48,1024]{2,1,0:T(8,128)S(1)} %shard_map.17) | data formatting | bytes 4718592
Async XLA Ops:
  0.0 1.9 %copy-start = (f32[12,6,8192]{2,1,0:T(8,128)S(1)}, f32[12,6,8192]{2,1,0:T(8,128)}, u32[]{:S(2)}) copy-start(f32[12,6,8192]{2,1,0:T(8,128)} %x_hbm.1) | copy-start | bytes 7077892

commit v3 on v2

--- a/solution.py
+++ b/solution.py
@@ -94,7 +94,8 @@
                 packed[k, dest, pl.ds(m, cut, stride=members), :] = jnp.where(mask, p, swap(q))
                 packed[k, dest, pl.ds(rows // 2 + m, cut, stride=members), :] = jnp.where(mask, swap(p), q)
 
-    for s, (k, half, _, _) in enumerate(stages):
+    def send_stage(s):
+        k, half, _, _ = stages[s]
 
         def block(n, _):
             to = lax.rem(a + tms // 2 + n, tms)
@@ -114,7 +115,7 @@
                     pl.semaphore_wait(barrier, devices - 1)
 
             def send(g, _):
-                dest = to * groups + lax.rem(b + g, groups)
+                dest = to * groups + lax.rem(b + g + 1, groups)
 
                 @pl.when(dest != me)
                 def _():
@@ -126,6 +127,10 @@
             return 0
 
         lax.fori_loop(0, tms, block, 0)
+
+    early = min(2, len(stages))
+    for s in range(early):
+        send_stage(s)
     for k in range(chunks):
         landed[k, me] = packed[k, me]
 
@@ -199,6 +204,9 @@
                             out_ref[i, j : j + 8, columns_of(k, b)] = got[i]
             if offset:
                 cov_copy(s, offset).start()
+            if offset == groups - 1 and s == 0:
+                for later in range(early, len(stages)):
+                    send_stage(later)
 
     if folded:
         s, k = len(stages) - 1, chunks - 1

time: 78.3 us -> 79.4 us (1.014)
  Pallas kernels: 74 us -> 75.3 us
    pallas_call x1, Pallas kernels: 74 us -> 75.3 us  [per_device(): pl.pallas_call(functools.partial(kernel, dims), out_shape=jax.ShapeDtypeS...]
where the time goes in v3:
time: 79.4 us; the launch traced here: 78.6 us
  Pallas kernels  75.3 us (95%)
  local copies, waits for them, and re-layouts  3.3 us (4%)
    pallas_call x1, Pallas kernels, per_device(): pl.pallas_call(functools.partial(kernel, dims), out_shape=jax.ShapeDtypeS...  75.3 us
    unnamed x3, local copies, waits for them, and re-layouts  3.3 us

profile of v3, /device:TPU:0, one launch (start us, length us, event | category | flops | bytes accessed | tf_op | source)
XLA Modules:
  0.0 78.6 jit_solution(18036600089822059275)
XLA Ops:
  0.0 0.0 copy-start
  0.0 1.9 %copy-done = f32[12,6,8192]{2,1,0:T(8,128)S(1)} copy-done((f32[12,6,8192]{2,1,0:T(8,128)S(1)}, f32[12,6,8192]{2,1,0:T(8,128)}, u32[]{:S(2)}) %copy-start) | copy-done | bytes 2359320
  1.9 75.3 %shard_map.17 = f32[12,48,1024]{2,1,0:T(8,128)S(1)} custom-call(f32[12,6,8192]{2,1,0:T(8,128)S(1)} %copy-done), custom_call_target="tpu_custom_call" | custom-call | tf_op jit(solution)/shard_map/pallas_call | solution.py:258
  77.2 1.4 %copy.3 = f32[12,48,1024]{2,1,0:T(8,128)} copy(f32[12,48,1024]{2,1,0:T(8,128)S(1)} %shard_map.17) | data formatting | bytes 4718592
Async XLA Ops:
  0.0 1.9 %copy-start = (f32[12,6,8192]{2,1,0:T(8,128)S(1)}, f32[12,6,8192]{2,1,0:T(8,128)}, u32[]{:S(2)}) copy-start(f32[12,6,8192]{2,1,0:T(8,128)} %x_hbm.1) | copy-start | bytes 7077892

commit v4 on v2

--- a/solution.py
+++ b/solution.py
@@ -114,7 +114,7 @@
                     pl.semaphore_wait(barrier, devices - 1)
 
             def send(g, _):
-                dest = to * groups + lax.rem(b + g, groups)
+                dest = to * groups + lax.rem(b + g + 1, groups)
 
                 @pl.when(dest != me)
                 def _():

time: 78.3 us -> 77.1 us (0.985); the launches traced: 77.3 us -> 76.9 us
  no operation moved by 1% of the time
where the time goes in v4:
time: 77.1 us; the launch traced here: 76.9 us
  Pallas kernels  73.6 us (95%)
  local copies, waits for them, and re-layouts  3.3 us (4%)
    pallas_call x1, Pallas kernels, per_device(): pl.pallas_call(functools.partial(kernel, dims), out_shape=jax.ShapeDtypeS...  73.6 us
    unnamed x3, local copies, waits for them, and re-layouts  3.3 us

profile of v4, /device:TPU:0, one launch (start us, length us, event | category | flops | bytes accessed | tf_op | source)
XLA Modules:
  0.0 76.9 jit_solution(5731048136825347125)
XLA Ops:
  0.0 0.0 copy-start
  0.0 1.9 %copy-done = f32[12,6,8192]{2,1,0:T(8,128)S(1)} copy-done((f32[12,6,8192]{2,1,0:T(8,128)S(1)}, f32[12,6,8192]{2,1,0:T(8,128)}, u32[]{:S(2)}) %copy-start) | copy-done | bytes 2359320
  1.9 73.6 %shard_map.17 = f32[12,48,1024]{2,1,0:T(8,128)S(1)} custom-call(f32[12,6,8192]{2,1,0:T(8,128)S(1)} %copy-done), custom_call_target="tpu_custom_call" | custom-call | tf_op jit(solution)/shard_map/pallas_call | solution.py:250
  75.5 1.4 %copy.3 = f32[12,48,1024]{2,1,0:T(8,128)} copy(f32[12,48,1024]{2,1,0:T(8,128)S(1)} %shard_map.17) | data formatting | bytes 4718592
Async XLA Ops:
  0.0 1.9 %copy-start = (f32[12,6,8192]{2,1,0:T(8,128)S(1)}, f32[12,6,8192]{2,1,0:T(8,128)}, u32[]{:S(2)}) copy-start(f32[12,6,8192]{2,1,0:T(8,128)} %x_hbm.1) | copy-start | bytes 7077892
